TPU v7x, 32 devices: a whole 2x2x4 slice. The times are simulated.
32 devices in a mesh: dp: 4 (over x, y), tp: 8 (over z, core).
Axes of the slice: x: 2, y: 2, z: 4, core: 2. Of those that a mesh axis runs over, the one named last changes fastest.
Arguments:
- x: bfloat16 [11264, 3072], P(('dp', 'tp')), parts along dimension 0
- dy: bfloat16 [11264, 3072], P(('dp', 'tp')), parts along dimension 0
- pre: bfloat16 [11264, 9216], P('dp', 'tp'), parts along dimension 0
- w_in: bfloat16 [3072, 9216], P(None, 'tp')
- w_down: bfloat16 [9216, 3072], P('tp')
Outputs:
- output 1: bfloat16 [11264, 3072], P(('dp', 'tp')), parts along dimension 0
- output 2: bfloat16 [12288, 9216], P('dp', 'tp'), parts along dimension 0
- output 3: bfloat16 [36864, 3072], P(('dp', 'tp')), parts along dimension 0
There are 4 independent parts. A program takes and returns all parts, laid end to end along the dimension named above; an argument that names none is the same for every part.
All inputs are finite; a program needn't handle non-finite values.
Results may differ from a plain program's by a relative error of at most 0.012.
Values are sent between devices in bfloat16 or wider.
A program may use at most 2 GiB of HBM per device.

v0:
```python
import jax
import jax.numpy as jnp


def act(pre):
    return jnp.square(jax.nn.relu(pre))


def solution(mesh):
    def step(x, dy, pre, w_in, w_down):
        hidden, back = jax.vjp(act, pre.astype(jnp.float32))
        d_hidden = jnp.dot(dy, w_down.T, preferred_element_type=jnp.float32)
        d_pre = back(d_hidden)[0].astype(jnp.bfloat16)
        dx = jnp.dot(d_pre, w_in.T)
        groups = mesh.shape["dp"]

        def by_group(a, b):
            a, b = (t.reshape(groups, -1, t.shape[-1]) for t in (a, b))
            product = jnp.einsum("gta,gtb->gab", a, b, preferred_element_type=jnp.float32)
            return product.astype(jnp.bfloat16).reshape(-1, b.shape[-1])

        return dx, by_group(x, d_pre), by_group(hidden.astype(jnp.bfloat16), dy)

    return step
```

profile of v0, /device:TPU:0, one launch (start us, length us, event | category | flops | bytes accessed | tf_op | source)
XLA Modules:
  0.0 504.6 jit_solution(11818538538069023916)
XLA Ops:
  7.2 0.0 all-gather.10.cloned.1.call-start
  7.2 0.7 all-gather.10.cloned.1.call-update
  7.9 0.0 all-gather.12.cloned.1.call-start
  7.9 0.7 all-gather.12.cloned.1.call-update
  8.6 0.0 reduce-scatter.4.cloned.1.call-start
  8.7 159.0 %all-gather.10.cloned.1.call-done = bf16[2816,3072]{1,0:T(8,128)(2,1)} async-done(((bf16[352,3072]{1,0:T(8,128)(2,1)}), bf16[2816,3072]{1,0:T(8,128)(2,1)}) %all-gather.10.cloned.1.call-update) | async-done | bytes 17301520 | tf_op args[1]
  167.7 28.6 %fusion.4 = bf16[2816,1152]{1,0:T(8,128)(2,1)S(1)} fusion(bf16[2816,1152]{1,0:T(8,128)(2,1)} %param, bf16[2816,3072]{1,0:T(8,128)(2,1)} %all-gather.10.cloned.1.call-done, bf16[1152,3072]{1,0:T(8,128)(2,1)} %param.2), kind=kOutput, calls=%fused_computation.9 | convolution fusion | flops 19954040832 | bytes 37355520 | tf_op jit(solution)/dot_general | solution.py:12
  196.3 0.0 copy-start
  196.3 2.8 copy-done
  199.1 27.8 %fusion.9 = bf16[2816,3072]{1,0:T(8,128)(2,1)} fusion(bf16[2816,1152]{1,0:T(8,128)(2,1)S(1)} %fusion.4, bf16[3072,1152]{1,0:T(8,128)(2,1)} %param.3), kind=kOutput, calls=%fused_computation.13 | convolution fusion | flops 19931332608 | bytes 30867456 | tf_op jit(solution)/dot_general | solution.py:14
  226.9 0.0 reduce-scatter.4.cloned.1.call-update
  227.0 96.5 %all-gather.12.cloned.1.call-done = bf16[2816,3072]{1,0:T(8,128)(2,1)} async-done(((bf16[352,3072]{1,0:T(8,128)(2,1)}), bf16[2816,3072]{1,0:T(8,128)(2,1)}) %all-gather.12.cloned.1.call-update) | async-done | bytes 17301520 | tf_op jit(solution)/reshape | solution.py:18
  323.5 26.5 %fusion.5 = bf16[3072,1152]{0,1:T(8,128)(2,1)} fusion(bf16[2816,1152]{1,0:T(8,128)(2,1)} %copy-done, bf16[2816,3072]{1,0:T(8,128)(2,1)} %all-gather.12.cloned.1.call-done), kind=kOutput, calls=%fused_computation.10 | convolution fusion | flops 19934871552 | bytes 30867456 | tf_op jit(solution)/gta,gtb->gab/dot_general | solution.py:19
  350.0 10.3 %copy = bf16[3072,1152]{1,0:T(8,128)(2,1)} copy(bf16[3072,1152]{0,1:T(8,128)(2,1)} %fusion.5) | data formatting | bytes 14155776
  360.3 26.8 %convolution_convert_fusion = bf16[1152,3072]{1,0:T(8,128)(2,1)} fusion(bf16[2816,3072]{1,0:T(8,128)(2,1)} %all-gather.10.cloned.1.call-done, bf16[2816,1152]{1,0:T(8,128)(2,1)} %param), kind=kOutput, calls=%fused_computation.7 | convolution fusion | flops 19947847680 | bytes 30867456 | tf_op jit(solution)/gta,gtb->gab/dot_general | solution.py:19
  387.0 111.1 %reduce-scatter.4.cloned.1.call-done = bf16[352,3072]{1,0:T(8,128)(2,1)} async-done(((bf16[2816,3072]{1,0:T(8,128)(2,1)}), bf16[352,3072]{1,0:T(8,128)(2,1)}) %reduce-scatter.4.cloned.1.call-update) | async-done | bytes 2162704
Async XLA Ops:
  7.2 160.5 %all-gather.10.cloned.1.call-start = ((), (), s32[]{:S(2)}) async-start(), calls=%async_computation.1 | async-start | bytes 19464192 | tf_op args[1]
  7.9 315.6 %all-gather.12.cloned.1.call-start = ((), (), s32[]{:S(2)}) async-start(), calls=%async_computation.2 | async-start | bytes 19464192 | tf_op jit(solution)/reshape | solution.py:18
  8.6 489.4 %reduce-scatter.4.cloned.1.call-start = ((), (), s32[]{:S(2)}) async-start(), calls=%async_computation.3 | async-start | bytes 19464192
  196.3 2.8 copy-start
Sparse Core Ops, SparseCore 0:
  9.6 158.0 all-gather.9
  169.3 154.0 all-gather.11
  326.4 171.6 reduce-scatter.3
where the time goes:
time: 505 us
  waiting for transfers between devices  368 us (73%)
  matrix products  110 us (22%)
  between operations  13.8 us (3%)
  local copies, waits for them, and re-layouts  13 us (3%)
    unnamed x5, waiting for transfers between devices  271 us
    reshape x1, waiting for transfers between devices, by_group(): a, b = (t.reshape(groups, -1, t.shape[-1]) for t in (a, b))  96.5 us
    dot_general x2, matrix products, by_group(): jnp.einsum('gta,gtb->gab', a, b, preferred_element_type=jnp.float32)  53.3 us
    dot_general x1, matrix products, step(): d_hidden = jnp.dot(dy, w_down.T, preferred_element_type=jnp.float32)  28.6 us
    dot_general x1, matrix products, step(): dx = jnp.dot(d_pre, w_in.T)  27.8 us
    unnamed x3, local copies, waits for them, and re-layouts  13 us
  transfers between devices with their start and end apart: 3, of which 3 were waited for; matrix products, arithmetic and copies ran while one was open for 24% of the time, Pallas kernels for 0%

commit v1 on v0

v1 whole, which is shorter than its diff:
```python
import functools

import jax
import jax.numpy as jnp
from jax import lax
from jax.experimental import pallas as pl
from jax.experimental.pallas import tpu as pltpu
from jax.sharding import PartitionSpec as P

MESH = pl.DeviceIdType.MESH
F32, BF16 = jnp.float32, jnp.bfloat16
NT = (((1,), (1,)), ((), ()))
CHIPS = 4


def tile(n):
    return next(t for t in (384, 256, 128) if n % t == 0)


def kernel(
    dy_ref, x_ref, pre_ref, wi_ref, wd_ref,
    dyf_ref, xf_ref, dpre_ref, finl_ref, finr_ref, own_ref,
    wd_v, wi_v, dp_v, dyb, preb, prt_v, lin_v, out_v, rs_v, fin_v, own_v,
    link_s, link_r, d2d_s, d2d_r, push_s, push_r, rs_s, rs_r, load_s, dpre_s, misc_s,
):
    me = lax.axis_index("tp")
    g = lax.axis_index("dp")
    z, c = me // 2, me % 2
    rows, d_model = dy_ref.shape
    half = rows // 2
    ff = wd_ref.shape[0]
    ins, fulls = (dy_ref, x_ref), (dyf_ref, xf_ref)
    first, last = z == 0, z == CHIPS - 1
    end, mid = (z == 0) | (z == 3), (z == 1) | (z == 2)
    partner = 2 * z + 1 - c

    def block(zb, core):
        return pl.ds(pl.multiple_of((2 * zb + core) * rows, 16), rows)

    def half_of(zb, core, h):
        return pl.ds(pl.multiple_of((2 * zb + core) * rows + h * half, 16), half)

    def neighbour(d):
        return 2 * (z - 1 if d == 0 else z + 1) + c

    def link(a, d, s, h, zb, own=False, to=None):
        dst = fulls[a].at[half_of(zb, c, h)]
        src = ins[a].at[pl.ds(h * half, half)] if own else dst
        return pltpu.make_async_remote_copy(
            src_ref=src, dst_ref=dst, send_sem=link_s.at[a, d, s, h], recv_sem=link_r.at[a, d, s, h],
            device_id=(g, neighbour(d) if to is None else to), device_id_type=MESH)

    def d2d(a, zb, h, own=False, core=None):
        core = c if core is None else core
        dst = fulls[a].at[half_of(zb, core, h)]
        src = ins[a].at[pl.ds(h * half, half)] if own else dst
        return pltpu.make_async_remote_copy(
            src_ref=src, dst_ref=dst, send_sem=d2d_s.at[a, zb, h], recv_sem=d2d_r.at[a, zb, h],
            device_id=(g, partner), device_id_type=MESH)

    def has_link(d):
        return z >= 1 if d == 0 else z <= 2

    def arrives(d, s):
        return z + s + 1 <= 3 if d == 0 else z - s - 1 >= 0

    def source(d, s):
        return z + s + 1 if d == 0 else z - s - 1

    def arrival(a, d, s, h):
        zb = source(d, s)
        link(a, d, s, h, zb, to=partner).wait_recv()
        if s < 2:
            @pl.when(has_link(d))
            def _():
                link(a, d, s + 1, h, zb).start()
        d2d(a, zb, h).start()

    def send_own(a, d):
        for h in range(2):
            link(a, d, 0, h, z, own=True).start()

    def push(zb):
        return pltpu.make_async_remote_copy(
            src_ref=out_v, dst_ref=prt_v.at[zb], send_sem=push_s, recv_sem=push_r.at[zb],
            device_id=(g, partner), device_id_type=MESH)

    def rs(d, s, to):
        return pltpu.make_async_remote_copy(
            src_ref=rs_v.at[s - 2], dst_ref=lin_v.at[d, s - 2], send_sem=rs_s.at[s - 2], recv_sem=rs_r.at[d, s - 2],
            device_id=(g, to), device_id_type=MESH)

    def local(src, dst, sem):
        return pltpu.make_async_copy(src, dst, sem)

    def dpre_block(slot, b):
        t = tile(ff)
        at = pl.ds(pl.multiple_of(b * rows, 16), rows)

        def body(j, _):
            cols = pl.ds(pl.multiple_of(j * t, 128), t)
            dh = lax.dot_general(dyb[slot], wd_v[cols, :], NT, preferred_element_type=F32)
            p = preb[slot, :, cols].astype(F32)
            dp_v[at, cols] = jnp.where(p > 0, dh * (2.0 * p), 0.0).astype(BF16)
            return 0

        lax.fori_loop(0, ff // t, body, 0)

    def dx_block(b, store, adds):
        t = tile(d_model)
        at = pl.ds(pl.multiple_of(b * rows, 16), rows)

        def body(j, _):
            cols = pl.ds(pl.multiple_of(j * t, 128), t)
            acc = lax.dot_general(dp_v[at, :], wi_v[cols, :], NT, preferred_element_type=F32)
            for add in adds:
                acc = acc + add[:, cols].astype(F32)
            store[:, cols] = acc.astype(store.dtype)
            return 0

        lax.fori_loop(0, d_model // t, body, 0)

    def dpre_out(b):
        at = pl.ds(pl.multiple_of(b * rows, 16), rows)
        return local(dp_v.at[at], dpre_ref.at[at], dpre_s.at[b])

    def load(slot, zb, core, src=None):
        at = block(zb, core)
        return (local(dyf_ref.at[at] if src is None else src, dyb.at[slot], load_s.at[slot, 0]),
                local(pre_ref.at[at], preb.at[slot], load_s.at[slot, 1]))

    def process(zb, own=False):
        for copy in load(0, zb, c, dy_ref if own else None):
            copy.start()
        for h in range(2):
            d2d(0, zb, h, core=1 - c).wait_recv()
        for copy in load(1, zb, 1 - c):
            copy.start()
        if own:
            local(wd_ref, wd_v, misc_s.at[0]).wait()
        for slot in range(2):
            for copy in load(slot, zb, c if slot == 0 else 1 - c, dy_ref if own and slot == 0 else None):
                copy.wait()
            b = 2 * zb + (c if slot == 0 else 1 - c)
            dpre_block(slot, b)
            dpre_out(b).start()
        if own:
            local(dyb.at[0], dyf_ref.at[block(z, c)], misc_s.at[2]).start()
            local(wi_ref, wi_v, misc_s.at[1]).wait()
            local(dyb.at[0], dyf_ref.at[block(z, c)], misc_s.at[2]).wait()
        else:
            push(zb).wait_send()
        dx_block(2 * zb + 1 - c, out_v, ())
        push(zb).start()

    def finish(d):
        for dd, ref in ((0, finl_ref), (1, finr_ref)):
            @pl.when(d == dd)
            def _():
                copy = local(fin_v, ref, misc_s.at[3])
                copy.start()
                copy.wait()

    main = jnp.where(z >= 2, 0, 1)
    other = 1 - main

    def chip_at(d, s):
        return z + s * (2 * d - 1)

    def sum_at(d, s, lin):
        zb = chip_at(d, s)
        push(zb).wait_recv()
        adds = [prt_v.at[zb]]
        if lin:
            rs(d, s + 1, partner).wait_recv()
            adds.append(lin_v.at[d, s - 1])
        dx_block(2 * zb + c, fin_v if s == 1 else rs_v.at[s - 2], adds)
        if s == 1:
            finish(d)
        else:
            rs(d, s, 2 * chip_at(d, 1) + c).start()

    barrier = pltpu.get_barrier_semaphore()
    pl.semaphore_signal(barrier, inc=1, device_id=(g, partner), device_id_type=MESH)
    for d in range(2):
        @pl.when(has_link(d))
        def _():
            pl.semaphore_signal(barrier, inc=1, device_id=(g, neighbour(d)), device_id_type=MESH)
    pl.semaphore_wait(barrier, jnp.where(end, 2, 3))

    for d in range(2):
        @pl.when(has_link(d))
        def _():
            send_own(0, d)
    for h in range(2):
        d2d(0, z, h, own=True).start()
    local(wd_ref, wd_v, misc_s.at[0]).start()
    local(wi_ref, wi_v, misc_s.at[1]).start()

    @pl.when(last)
    def _():
        send_own(1, 0)

    @pl.when(first)
    def _():
        send_own(1, 1)

    for h in range(2):
        d2d(1, z, h, own=True).start()
    process(z, own=True)
    copy = local(x_ref, fin_v, misc_s.at[3])
    copy.start()
    copy.wait()
    copy = local(fin_v, xf_ref.at[block(z, c)], misc_s.at[3])
    copy.start()
    copy.wait()
    push(z).wait_recv()
    dx_block(2 * z + c, own_v, (prt_v.at[z],))
    local(own_v, own_ref, misc_s.at[4]).start()

    for h in range(2):
        for d in range(2):
            @pl.when(arrives(d, 0))
            def _():
                arrival(0, d, 0, h)

    @pl.when(z == 2)
    def _():
        send_own(1, 0)

    @pl.when(z == 1)
    def _():
        send_own(1, 1)

    def near(i, _):
        process(jnp.where(first, 1, jnp.where(last, 2, z - 1 + 2 * i)))
        return 0

    lax.fori_loop(0, jnp.where(end, 1, 2), near, 0)

    @pl.when(end)
    def _():
        sum_at(main, 1, False)

    for h in range(2):
        for d in range(2):
            @pl.when(arrives(d, 1))
            def _():
                arrival(0, d, 1, h)

    @pl.when(z == 1)
    def _():
        send_own(1, 0)

    @pl.when(z == 2)
    def _():
        send_own(1, 1)

    def x_in(zz, d, s):
        @pl.when(z == zz)
        def _():
            for h in range(2):
                arrival(1, d, s, h)

    process(jnp.where(z < 2, z + 2, z - 2))

    @pl.when(end)
    def _():
        sum_at(main, 2, False)

    x_in(1, 1, 0)
    x_in(2, 0, 0)

    @pl.when(end)
    def _():
        for h in range(2):
            for d in range(2):
                @pl.when(arrives(d, 2))
                def _():
                    arrival(0, d, 2, h)
        process(3 - z)
        sum_at(main, 3, False)

    x_in(1, 0, 0)
    x_in(2, 1, 0)

    @pl.when(mid)
    def _():
        sum_at(main, 1, True)

    x_in(1, 0, 1)
    x_in(2, 1, 1)
    x_in(0, 0, 0)
    x_in(3, 1, 0)

    @pl.when(mid)
    def _():
        sum_at(main, 2, True)

    x_in(0, 0, 1)
    x_in(3, 1, 1)

    @pl.when(mid)
    def _():
        sum_at(other, 1, True)

    x_in(0, 0, 2)
    x_in(3, 1, 2)

    for zb in range(CHIPS):
        for h in range(2):
            d2d(1, zb, h, core=1 - c).wait_recv()
            for a in range(2):
                d2d(a, zb, h).wait_send()
    for a in range(2):
        for d in range(2):
            for s in range(3):
                sent = has_link(d) if s == 0 else has_link(d) & arrives(d, s - 1)

                @pl.when(sent)
                def _():
                    for h in range(2):
                        link(a, d, s, h, z).wait_send()
    push(z).wait_send()
    rs(main, 2, partner).wait_send()

    @pl.when(end)
    def _():
        rs(main, 3, partner).wait_send()

    for b in range(2 * CHIPS):
        dpre_out(b).wait()
    local(own_v, own_ref, misc_s.at[4]).wait()


def gather_and_sum(dy, x, pre, w_in, w_down):
    rows, d_model = dy.shape
    tokens, ff = pre.shape
    out = jax.ShapeDtypeStruct
    dma = pltpu.SemaphoreType.DMA
    flops = 4 * tokens * d_model * ff
    return pl.pallas_call(
        kernel,
        out_shape=(out((tokens, d_model), BF16), out((tokens, d_model), BF16), out((tokens, ff), BF16),
                   out((rows, d_model), BF16), out((rows, d_model), BF16), out((rows, d_model), F32)),
        in_specs=[pl.BlockSpec(memory_space=pl.ANY)] * 5,
        out_specs=(pl.BlockSpec(memory_space=pl.ANY),) * 6,
        scratch_shapes=[
            pltpu.VMEM((ff, d_model), BF16),
            pltpu.VMEM((d_model, ff), BF16),
            pltpu.VMEM((tokens, ff), BF16),
            pltpu.VMEM((2, rows, d_model), BF16),
            pltpu.VMEM((2, rows, ff), BF16),
            pltpu.VMEM((CHIPS, rows, d_model), BF16),
            pltpu.VMEM((2, 2, rows, d_model), BF16),
            pltpu.VMEM((rows, d_model), BF16),
            pltpu.VMEM((2, rows, d_model), BF16),
            pltpu.VMEM((rows, d_model), BF16),
            pltpu.VMEM((rows, d_model), F32),
            dma((2, 2, 3, 2)), dma((2, 2, 3, 2)), dma((2, CHIPS, 2)), dma((2, CHIPS, 2)),
            dma, dma((CHIPS,)), dma((2,)), dma((2, 2)), dma((2, 2)), dma((2 * CHIPS,)), dma((5,)),
        ],
        compiler_params=pltpu.CompilerParams(
            collective_id=0, has_side_effects=True, vmem_limit_bytes=66_000_000),
        cost_estimate=pl.CostEstimate(flops=flops, bytes_accessed=8 * tokens * d_model, transcendentals=0),
        name="gather_and_sum",
    )(dy, x, pre, w_in, w_down)


def solution(mesh):
    def step(x, dy, pre, w_in, w_down):
        dyf, xf, d_pre, fin_l, fin_r, own = gather_and_sum(dy, x, pre, w_in, w_down)
        n = 2 * CHIPS
        from_right = lax.ppermute(fin_l, "tp", [(i, i - 2) for i in range(2, n)])
        from_left = lax.ppermute(fin_r, "tp", [(i, i + 2) for i in range(n - 2)])
        hidden = jnp.square(jax.nn.relu(pre.astype(F32))).astype(BF16)
        over_tokens = (((0,), (0,)), ((), ()))
        dw_in = lax.dot_general(xf, d_pre, over_tokens, preferred_element_type=F32).astype(BF16)
        dw_down = lax.dot_general(hidden, dyf, over_tokens, preferred_element_type=F32).astype(BF16)
        dx = (own + from_right.astype(F32) + from_left.astype(F32)).astype(BF16)
        return dx, dw_in, dw_down

    rows = P(("dp", "tp"), None)
    return jax.shard_map(
        step, mesh=mesh,
        in_specs=(rows, rows, P("dp", "tp"), P(None, "tp"), P("tp", None)),
        out_specs=(rows, P("dp", "tp"), rows), check_vma=False)
```

time: 505 us -> 350 us (0.69)
  waiting for transfers between devices: 368 us -> 0.01 us
  Pallas kernels: 0 us -> 287 us
  matrix products: 110 us -> 53.9 us
  between operations: 13.8 us -> 0.67 us
  local copies, waits for them, and re-layouts: 13 us -> 0.01 us
  starting transfers between devices: 0.11 us -> 6.16 us
    pallas_call x0 -> x1, Pallas kernels: none -> 287 us  [gather_and_sum(): pl.pallas_call(kernel, out_shape=(out((tokens, d_model), BF16), out((toke...]
    unnamed x5 -> x0, waiting for transfers between devices: 271 us -> none
    reshape x1 -> x0, waiting for transfers between devices: 96.5 us -> none  [by_group(): a, b = (t.reshape(groups, -1, t.shape[-1]) for t in (a, b))]
    dot_general x4 -> x2, matrix products: 110 us -> 53.9 us  [the longest x1 28.9 us: step(): lax.dot_general(xf, d_pre, over_tokens, preferred_element_type=F32)]
    unnamed x3 -> x4, local copies, waits for them, and re-layouts: 13 us -> 0.01 us
    ppermute x0 -> x2, starting transfers between devices: none -> 6.16 us  [the longest x1 4.86 us: step(): from_left = lax.ppermute(fin_r, 'tp', [(i, i + 2) for i in range(n - 2)])]
  transfers between devices with their start and end apart: 3 -> 2, of which waited for: 3 -> 0; matrix products, arithmetic and copies ran while one was open for 24% -> 15% of each run, Pallas kernels for 0% -> 0%
where the time goes in v1:
time: 350 us
  Pallas kernels  287 us (82%)
  matrix products  53.9 us (15%)
  starting transfers between devices  6.16 us (2%)
    pallas_call x1, Pallas kernels, gather_and_sum(): pl.pallas_call(kernel, out_shape=(out((tokens, d_model), BF16), out((toke...  287 us
    dot_general x1, matrix products, step(): lax.dot_general(xf, d_pre, over_tokens, preferred_element_type=F32)  28.9 us
    dot_general x1, matrix products, step(): lax.dot_general(hidden, dyf, over_tokens, preferred_element_type=F32)  25 us
  transfers between devices with their start and end apart: 2, of which 0 were waited for; matrix products, arithmetic and copies ran while one was open for 15% of the time, Pallas kernels for 0%

profile of v1, /device:TPU:0, one launch (start us, length us, event | category | flops | bytes accessed | tf_op | source)
XLA Modules:
  0.0 349.5 jit_solution(11660697034273659039)
XLA Ops:
  0.6 286.5 %gather_and_sum.1 = (bf16[2816,3072]{1,0:T(8,128)(2,1)}, bf16[2816,3072]{1,0:T(8,128)(2,1)}, bf16[2816,1152]{1,0:T(8,128)(2,1)}, bf16[352,3072]{1,0:T(8,128)(2,1...) custom-call(bf16[352,3072]{1,0:T(8,128)(2,1)} %dy_ref.1, bf16[352,3072]{1,0:T(8,128)(2,1)} %x_ref.1, ...), custom_call_target="tpu_custom_call" | custom-call | flops 39862665216 | bytes 69206016 | tf_op jit(solution)/shard_map/gather_and_sum/pallas_call | solution.py:342
  287.2 1.3 collective-permute-start
  288.5 4.9 %collective-permute-start.1 = (bf16[352,3072]{1,0:T(8,128)(2,1)}, bf16[352,3072]{1,0:T(8,128)(2,1)S(1)}, u32[]{:S(2)}, u32[]{:S(2)}) collective-permute-start(bf16[352,3072]{1,0:T(8,128)(2,1)} %get-tuple-element.11), channel_id=1, source_target_pairs={{0,2},{1,3},{2,4},{3,5},{4,6},{5,7},{8,10},{9,11},{10,12},{11,13},... | collective-permute-start | bytes 6488072 | tf_op jit(solution)/shard_map/ppermute | solution.py:375
  293.3 0.0 copy-start.1
  293.3 28.9 %convolution_convert_fusion.1 = bf16[3072,1152]{1,0:T(8,128)(2,1)} fusion(bf16[2816,3072]{1,0:T(8,128)(2,1)} %get-tuple-element.12, bf16[2816,1152]{1,0:T(8,128)(2,1)} %get-tuple-element.13), kind=kOutput, calls=%fused_computation.2 | convolution fusion | flops 19934871552 | bytes 30867456 | tf_op jit(solution)/shard_map/dot_general | solution.py:378
  322.3 0.0 copy-done.1
  322.3 0.0 copy-start
  322.3 25.0 %convolution_convert_fusion = bf16[1152,3072]{1,0:T(8,128)(2,1)} fusion(bf16[2816,3072]{1,0:T(8,128)(2,1)} %get-tuple-element.14, bf16[2816,1152]{1,0:T(8,128)(2,1)S(1)} %copy-done.1), kind=kOutput, calls=%fused_computation.1 | convolution fusion | flops 19947847680 | bytes 30867456 | tf_op jit(solution)/shard_map/dot_general | solution.py:379
  347.2 0.0 collective-permute-done
  347.3 0.0 collective-permute-done.1
  347.3 0.0 copy-done
  347.3 2.3 add_convert_fusion
Async XLA Ops:
  287.2 60.1 %collective-permute-start = (bf16[352,3072]{1,0:T(8,128)(2,1)}, bf16[352,3072]{1,0:T(8,128)(2,1)S(1)}, u32[]{:S(2)}, u32[]{:S(2)}) collective-permute-start(bf16[352,3072]{1,0:T(8,128)(2,1)} %get-tuple-element.10), channel_id=1, source_target_pairs={{2,0},{3,1},{4,2},{5,3},{6,4},{7,5},{10,8},{11,9},{12,10},{13,11},... | collective-permute-start | bytes 6488072 | tf_op jit(solution)/shard_map/ppermute | solution.py:374
  288.5 58.8 %collective-permute-start.1 = (bf16[352,3072]{1,0:T(8,128)(2,1)}, bf16[352,3072]{1,0:T(8,128)(2,1)S(1)}, u32[]{:S(2)}, u32[]{:S(2)}) collective-permute-start(bf16[352,3072]{1,0:T(8,128)(2,1)} %get-tuple-element.11), channel_id=1, source_target_pairs={{0,2},{1,3},{2,4},{3,5},{4,6},{5,7},{8,10},{9,11},{10,12},{11,13},... | collective-permute-start | bytes 6488072 | tf_op jit(solution)/shard_map/ppermute | solution.py:375
  293.3 28.9 %copy-start.1 = (bf16[2816,1152]{1,0:T(8,128)(2,1)S(1)}, bf16[2816,1152]{1,0:T(8,128)(2,1)}, u32[]{:S(2)}) copy-start(bf16[2816,1152]{1,0:T(8,128)(2,1)} %pre_ref.1) | copy-start | bytes 19464196
  322.3 25.0 %copy-start = (f32[352,3072]{1,0:T(8,128)S(1)}, f32[352,3072]{1,0:T(8,128)}, u32[]{:S(2)}) copy-start(f32[352,3072]{1,0:T(8,128)} %get-tuple-element.9) | copy-start | bytes 12976132

commit v2 on v1

--- a/solution.py
+++ b/solution.py
@@ -10,6 +10,7 @@
 MESH = pl.DeviceIdType.MESH
 F32, BF16 = jnp.float32, jnp.bfloat16
 NT = (((1,), (1,)), ((), ()))
+TN = (((0,), (0,)), ((), ()))
 CHIPS = 4
 
 
@@ -19,15 +20,16 @@
 
 def kernel(
     dy_ref, x_ref, pre_ref, wi_ref, wd_ref,
-    dyf_ref, xf_ref, dpre_ref, finl_ref, finr_ref, own_ref,
-    wd_v, wi_v, dp_v, dyb, preb, prt_v, lin_v, out_v, rs_v, fin_v, own_v,
-    link_s, link_r, d2d_s, d2d_r, push_s, push_r, rs_s, rs_r, load_s, dpre_s, misc_s,
+    dyf_ref, xf_ref, dpre_ref, fina_ref, finb_ref, own_ref, dwd_ref,
+    wd_v, wi_v, dp_v, dyb, preb, prt_v, lin_v, out_v, rs_v, fin_v, acc_v,
+    link_s, link_r, d2d_s, d2d_r, push_s, push_r, rs_s, rs_r, load_s, dpre_s, misc_s, dwd_s,
 ):
     me = lax.axis_index("tp")
     g = lax.axis_index("dp")
     z, c = me // 2, me % 2
     rows, d_model = dy_ref.shape
-    half = rows // 2
+    short = max(16, rows * 2 // 11 // 16 * 16)
+    sizes = ((rows // 2, rows - rows // 2), (rows - short, short))
     ff = wd_ref.shape[0]
     ins, fulls = (dy_ref, x_ref), (dyf_ref, xf_ref)
     first, last = z == 0, z == CHIPS - 1
@@ -37,23 +39,23 @@
     def block(zb, core):
         return pl.ds(pl.multiple_of((2 * zb + core) * rows, 16), rows)
 
-    def half_of(zb, core, h):
-        return pl.ds(pl.multiple_of((2 * zb + core) * rows + h * half, 16), half)
+    def half_of(a, zb, core, h):
+        return pl.ds(pl.multiple_of((2 * zb + core) * rows + h * sizes[a][0], 16), sizes[a][h])
 
     def neighbour(d):
         return 2 * (z - 1 if d == 0 else z + 1) + c
 
     def link(a, d, s, h, zb, own=False, to=None):
-        dst = fulls[a].at[half_of(zb, c, h)]
-        src = ins[a].at[pl.ds(h * half, half)] if own else dst
+        dst = fulls[a].at[half_of(a, zb, c, h)]
+        src = ins[a].at[pl.ds(h * sizes[a][0], sizes[a][h])] if own else dst
         return pltpu.make_async_remote_copy(
             src_ref=src, dst_ref=dst, send_sem=link_s.at[a, d, s, h], recv_sem=link_r.at[a, d, s, h],
             device_id=(g, neighbour(d) if to is None else to), device_id_type=MESH)
 
     def d2d(a, zb, h, own=False, core=None):
         core = c if core is None else core
-        dst = fulls[a].at[half_of(zb, core, h)]
-        src = ins[a].at[pl.ds(h * half, half)] if own else dst
+        dst = fulls[a].at[half_of(a, zb, core, h)]
+        src = ins[a].at[pl.ds(h * sizes[a][0], sizes[a][h])] if own else dst
         return pltpu.make_async_remote_copy(
             src_ref=src, dst_ref=dst, send_sem=d2d_s.at[a, zb, h], recv_sem=d2d_r.at[a, zb, h],
             device_id=(g, partner), device_id_type=MESH)
@@ -153,13 +155,56 @@
         dx_block(2 * zb + 1 - c, out_v, ())
         push(zb).start()
 
-    def finish(d):
-        for dd, ref in ((0, finl_ref), (1, finr_ref)):
-            @pl.when(d == dd)
+    def finish(ref):
+        copy = local(fin_v, ref, misc_s.at[3])
+        copy.start()
+        copy.wait()
+
+    def dw_down_rows(m):
+        t, tn = tile(ff), 512 if d_model % 512 == 0 else tile(d_model)
+        cols = pl.ds(m * t, t)
+
+        def loads(b, slot):
+            at = pl.ds(pl.multiple_of(b * rows, 16), rows)
+            return (local(dyf_ref.at[at], dyb.at[slot], load_s.at[slot, 0]),
+                    local(pre_ref.at[at, cols], preb.at[slot, :, pl.ds(0, t)], load_s.at[slot, 1]))
+
+        for copy in loads(0, 0):
+            copy.start()
+        acc_v[...] = jnp.zeros_like(acc_v)
+
+        def token_block(b, _):
+            slot = b % 2
+
+            @pl.when(b + 1 < 2 * CHIPS)
             def _():
-                copy = local(fin_v, ref, misc_s.at[3])
-                copy.start()
+                for copy in loads(b + 1, 1 - slot):
+                    copy.start()
+
+            for copy in loads(b, slot):
                 copy.wait()
+            hidden = jnp.square(jnp.maximum(preb[slot, :, pl.ds(0, t)].astype(F32), 0.0)).astype(BF16)
+
+            def body(n, _):
+                at = pl.ds(pl.multiple_of(n * tn, 128), tn)
+                acc_v[:, at] += lax.dot_general(hidden, dyb[slot, :, at], TN, preferred_element_type=F32)
+                return 0
+
+            return lax.fori_loop(0, d_model // tn, body, 0)
+
+        lax.fori_loop(0, 2 * CHIPS, token_block, 0)
+
+        def body(n, _):
+            at = pl.ds(pl.multiple_of(n * tn, 128), tn)
+            wd_v[cols, at] = acc_v[:, at].astype(BF16)
+            return 0
+
+        lax.fori_loop(0, d_model // tn, body, 0)
+        dw_down_out(m).start()
+
+    def dw_down_out(m):
+        at = pl.ds(m * tile(ff), tile(ff))
+        return local(wd_v.at[at], dwd_ref.at[at], dwd_s.at[m])
 
     main = jnp.where(z >= 2, 0, 1)
     other = 1 - main
@@ -167,7 +212,7 @@
     def chip_at(d, s):
         return z + s * (2 * d - 1)
 
-    def sum_at(d, s, lin):
+    def sum_at(d, s, lin, ref=None):
         zb = chip_at(d, s)
         push(zb).wait_recv()
         adds = [prt_v.at[zb]]
@@ -176,7 +221,7 @@
             adds.append(lin_v.at[d, s - 1])
         dx_block(2 * zb + c, fin_v if s == 1 else rs_v.at[s - 2], adds)
         if s == 1:
-            finish(d)
+            finish(ref)
         else:
             rs(d, s, 2 * chip_at(d, 1) + c).start()
 
@@ -215,6 +260,7 @@
     copy.start()
     copy.wait()
     push(z).wait_recv()
+    own_v = acc_v.at[pl.ds(0, rows)]
     dx_block(2 * z + c, own_v, (prt_v.at[z],))
     local(own_v, own_ref, misc_s.at[4]).start()
 
@@ -240,7 +286,7 @@
 
     @pl.when(end)
     def _():
-        sum_at(main, 1, False)
+        sum_at(main, 1, False, fina_ref)
 
     for h in range(2):
         for d in range(2):
@@ -286,7 +332,11 @@
 
     @pl.when(mid)
     def _():
-        sum_at(main, 1, True)
+        sum_at(main, 1, True, finb_ref)
+
+    local(own_v, own_ref, misc_s.at[4]).wait()
+    pieces = list(range(ff // tile(ff)))
+    dw_down_rows(pieces.pop(0))
 
     x_in(1, 0, 1)
     x_in(2, 1, 1)
@@ -297,12 +347,16 @@
     def _():
         sum_at(main, 2, True)
 
+    if pieces:
+        dw_down_rows(pieces.pop(0))
     x_in(0, 0, 1)
     x_in(3, 1, 1)
+    while pieces:
+        dw_down_rows(pieces.pop(0))
 
     @pl.when(mid)
     def _():
-        sum_at(other, 1, True)
+        sum_at(other, 1, True, fina_ref)
 
     x_in(0, 0, 2)
     x_in(3, 1, 2)
@@ -330,7 +384,8 @@
 
     for b in range(2 * CHIPS):
         dpre_out(b).wait()
-    local(own_v, own_ref, misc_s.at[4]).wait()
+    for m in range(ff // tile(ff)):
+        dw_down_out(m).wait()
 
 
 def gather_and_sum(dy, x, pre, w_in, w_down):
@@ -338,13 +393,14 @@
     tokens, ff = pre.shape
     out = jax.ShapeDtypeStruct
     dma = pltpu.SemaphoreType.DMA
-    flops = 4 * tokens * d_model * ff
+    flops = 6 * tokens * d_model * ff
     return pl.pallas_call(
         kernel,
         out_shape=(out((tokens, d_model), BF16), out((tokens, d_model), BF16), out((tokens, ff), BF16),
-                   out((rows, d_model), BF16), out((rows, d_model), BF16), out((rows, d_model), F32)),
+                   out((rows, d_model), BF16), out((rows, d_model), BF16), out((rows, d_model), F32),
+                   out((ff, d_model), BF16)),
         in_specs=[pl.BlockSpec(memory_space=pl.ANY)] * 5,
-        out_specs=(pl.BlockSpec(memory_space=pl.ANY),) * 6,
+        out_specs=(pl.BlockSpec(memory_space=pl.ANY),) * 7,
         scratch_shapes=[
             pltpu.VMEM((ff, d_model), BF16),
             pltpu.VMEM((d_model, ff), BF16),
@@ -356,9 +412,9 @@
             pltpu.VMEM((rows, d_model), BF16),
             pltpu.VMEM((2, rows, d_model), BF16),
             pltpu.VMEM((rows, d_model), BF16),
-            pltpu.VMEM((rows, d_model), F32),
+            pltpu.VMEM((max(rows, tile(ff)), d_model), F32),
             dma((2, 2, 3, 2)), dma((2, 2, 3, 2)), dma((2, CHIPS, 2)), dma((2, CHIPS, 2)),
-            dma, dma((CHIPS,)), dma((2,)), dma((2, 2)), dma((2, 2)), dma((2 * CHIPS,)), dma((5,)),
+            dma, dma((CHIPS,)), dma((2,)), dma((2, 2)), dma((2, 2)), dma((2 * CHIPS,)), dma((5,)), dma((ff // tile(ff),)),
         ],
         compiler_params=pltpu.CompilerParams(
             collective_id=0, has_side_effects=True, vmem_limit_bytes=66_000_000),
@@ -367,17 +423,28 @@
     )(dy, x, pre, w_in, w_down)
 
 
+def copy_kernel(src, dst):
+    dst[...] = src[...]
+
+
+def copied(a):
+    rows, cols = a.shape
+    block = pl.BlockSpec((rows // 9 if rows % 9 == 0 else rows, cols), lambda i: (i, 0))
+    return pl.pallas_call(
+        copy_kernel, out_shape=jax.ShapeDtypeStruct(a.shape, a.dtype), grid=(9 if rows % 9 == 0 else 1,),
+        in_specs=[block], out_specs=block,
+        cost_estimate=pl.CostEstimate(flops=rows * cols * 500, bytes_accessed=4 * rows * cols, transcendentals=0),
+        compiler_params=pltpu.CompilerParams(vmem_limit_bytes=16_000_000), name="copied")(a)
+
+
 def solution(mesh):
     def step(x, dy, pre, w_in, w_down):
-        dyf, xf, d_pre, fin_l, fin_r, own = gather_and_sum(dy, x, pre, w_in, w_down)
-        n = 2 * CHIPS
-        from_right = lax.ppermute(fin_l, "tp", [(i, i - 2) for i in range(2, n)])
-        from_left = lax.ppermute(fin_r, "tp", [(i, i + 2) for i in range(n - 2)])
-        hidden = jnp.square(jax.nn.relu(pre.astype(F32))).astype(BF16)
-        over_tokens = (((0,), (0,)), ((), ()))
-        dw_in = lax.dot_general(xf, d_pre, over_tokens, preferred_element_type=F32).astype(BF16)
-        dw_down = lax.dot_general(hidden, dyf, over_tokens, preferred_element_type=F32).astype(BF16)
-        dx = (own + from_right.astype(F32) + from_left.astype(F32)).astype(BF16)
+        _, xf, d_pre, fin_a, fin_b, own, dw_down = gather_and_sum(dy, x, pre, w_in, w_down)
+        a = lax.ppermute(fin_a, "tp", [(i, i ^ 2) for i in range(2 * CHIPS)])
+        b = lax.ppermute(fin_b, "tp", [(i, i ^ 6) for i in range(2, 6)])
+        dw_down = copied(dw_down)
+        dw_in = lax.dot_general(xf, d_pre, TN, preferred_element_type=F32).astype(BF16)
+        dx = (own + a.astype(F32) + b.astype(F32)).astype(BF16)
         return dx, dw_in, dw_down
 
     rows = P(("dp", "tp"), None)

time: 350 us -> 339 us (0.969)
  matrix products: 53.9 us -> 27.4 us
  waiting for transfers between devices: 0.01 us -> 12.7 us
  starting transfers between devices: 6.16 us -> 0.87 us
  local copies, waits for them, and re-layouts: 0.01 us -> 3.69 us
    dot_general x2 -> x1, matrix products: 53.9 us -> 27.4 us  [step(): lax.dot_general(xf, d_pre, TN, preferred_element_type=F32).astype(BF16)]
    ppermute x2, waiting for transfers between devices: 0.01 us -> 12.7 us  [the longest x1 12.7 us: step(): a = lax.ppermute(fin_a, 'tp', [(i, i ^ 2) for i in range(2 * CHIPS)])]
    ppermute x2, starting transfers between devices: 6.16 us -> 0.87 us  [the longest x1 0.8 us: step(): b = lax.ppermute(fin_b, 'tp', [(i, i ^ 6) for i in range(2, 6)])]
    pallas_call x0 -> x1, Pallas kernels: none -> 4.64 us  [copied(): pl.pallas_call(copy_kernel, out_shape=jax.ShapeDtypeStruct(a.shape, a.dty...]
    unnamed x4 -> x8, local copies, waits for them, and re-layouts: 0.01 us -> 3.69 us
  transfers between devices with their start and end apart: 2 -> 2, of which waited for: 0 -> 1; matrix products, arithmetic and copies ran while one was open for 15% -> 8% of each run, Pallas kernels for 0% -> 1%
where the time goes in v2:
time: 339 us; the launch traced here: 338 us
  Pallas kernels  290 us (86%)
  matrix products  27.4 us (8%)
  waiting for transfers between devices  12.7 us (4%)
  local copies, waits for them, and re-layouts  3.69 us (1%)
    pallas_call x1, Pallas kernels, gather_and_sum(): pl.pallas_call(kernel, out_shape=(out((tokens, d_model), BF16), out((toke...  286 us
    dot_general x1, matrix products, step(): lax.dot_general(xf, d_pre, TN, preferred_element_type=F32).astype(BF16)  27.4 us
    ppermute x1, waiting for transfers between devices, step(): a = lax.ppermute(fin_a, 'tp', [(i, i ^ 2) for i in range(2 * CHIPS)])  12.7 us
  transfers between devices with their start and end apart: 2, of which 1 were waited for; matrix products, arithmetic and copies ran while one was open for 8% of the time, Pallas kernels for 1%

profile of v2, /device:TPU:0, one launch (start us, length us, event | category | flops | bytes accessed | tf_op | source)
XLA Modules:
  0.0 337.9 jit_solution(12354979313953058613)
XLA Ops:
  0.6 285.6 %gather_and_sum.1 = (bf16[2816,3072]{1,0:T(8,128)(2,1)}, bf16[2816,3072]{1,0:T(8,128)(2,1)}, bf16[2816,1152]{1,0:T(8,128)(2,1)}, bf16[352,3072]{1,0:T(8,128)(2,1...) custom-call(bf16[352,3072]{1,0:T(8,128)(2,1)} %dy_ref.1, bf16[352,3072]{1,0:T(8,128)(2,1)} %x_ref.1, ...), custom_call_target="tpu_custom_call" | custom-call | flops 59793997824 | bytes 69206016 | tf_op jit(solution)/shard_map/gather_and_sum/pallas_call | solution.py:397
  286.2 0.1 collective-permute-start
  286.3 0.8 collective-permute-start.1
  287.1 0.0 copy-start
  287.1 3.0 copy-done
  290.1 0.0 copy-start.1
  290.1 0.0 slice-start
  290.1 4.6 %copied.1 = bf16[1152,3072]{1,0:T(8,128)(2,1)} custom-call(bf16[1152,3072]{1,0:T(8,128)(2,1)S(1)} %copy-done), custom_call_target="tpu_custom_call" | custom-call | flops 1769472000 | bytes 14155776 | tf_op jit(solution)/shard_map/copied/pallas_call | solution.py:433
  294.7 0.7 copy-done.1
  295.4 0.0 slice-start.1
  295.4 27.4 %convolution_convert_fusion = bf16[3072,1152]{1,0:T(8,128)(2,1)} fusion(bf16[2816,3072]{1,0:T(8,128)(2,1)} %get-tuple-element.12, bf16[2816,1152]{1,0:T(8,128)(2,1)S(1)} %copy-done.1), kind=kOutput, calls=%fused_computation | convolution fusion | flops 19934871552 | bytes 30867456 | tf_op jit(solution)/shard_map/dot_general | solution.py:446
  322.9 12.7 %collective-permute-done = bf16[352,3072]{1,0:T(8,128)(2,1)S(1)} collective-permute-done((bf16[352,3072]{1,0:T(8,128)(2,1)}, bf16[352,3072]{1,0:T(8,128)(2,1)S(1)}, u32[]{:S(2)}, u32[]{:S(2)}) %collective-permute-start) | collective-permute-done | bytes 2162720 | tf_op jit(solution)/shard_map/ppermute | solution.py:443
  335.5 0.0 collective-permute-done.1
  335.5 0.0 slice-done
  335.5 0.0 slice-done.1
  335.6 2.3 add_convert_fusion
  (1 shorter events, 0.0 us)
Async XLA Ops:
  286.2 49.3 %collective-permute-start = (bf16[352,3072]{1,0:T(8,128)(2,1)}, bf16[352,3072]{1,0:T(8,128)(2,1)S(1)}, u32[]{:S(2)}, u32[]{:S(2)}) collective-permute-start(bf16[352,3072]{1,0:T(8,128)(2,1)} %get-tuple-element.10), channel_id=1, source_target_pairs={{0,2},{1,3},{2,0},{3,1},{4,6},{5,7},{6,4},{7,5},{8,10},{9,11},{10,... | collective-permute-start | bytes 6488072 | tf_op jit(solution)/shard_map/ppermute | solution.py:443
  286.3 49.3 %collective-permute-start.1 = (bf16[352,3072]{1,0:T(8,128)(2,1)}, bf16[352,3072]{1,0:T(8,128)(2,1)S(1)}, u32[]{:S(2)}, u32[]{:S(2)}) collective-permute-start(bf16[352,3072]{1,0:T(8,128)(2,1)} %get-tuple-element.11), channel_id=1, source_target_pairs={{2,4},{3,5},{4,2},{5,3},{10,12},{11,13},{12,10},{13,11},{18,20},{1... | collective-permute-start | bytes 6488072 | tf_op jit(solution)/shard_map/ppermute | solution.py:444
  287.1 3.0 copy-start
  290.1 5.3 %copy-start.1 = (bf16[2816,1152]{1,0:T(8,128)(2,1)S(1)}, bf16[2816,1152]{1,0:T(8,128)(2,1)}, u32[]{:S(2)}) copy-start(bf16[2816,1152]{1,0:T(8,128)(2,1)} %get-tuple-element.13) | copy-start | bytes 19464196
  290.1 45.4 %slice-start = ((s8[4325376]{0:T(1024)(128)(4,1)}), s8[4194304]{0:T(1024)(128)(4,1)S(1)}, s32[]{:S(2)}) async-start(s8[4325376]{0:T(1024)(128)(4,1)} %bitcast.2), calls=%async_computation | async-start | bytes 8388608
  295.4 40.1 %slice-start.1 = ((s8[4325376]{0:T(1024)(128)(4,1)}), s8[131072]{0:T(1024)(128)(4,1)S(1)}, s32[]{:S(2)}) async-start(s8[4325376]{0:T(1024)(128)(4,1)} %bitcast.2), calls=%async_computation.1 | async-start | bytes 262144

commit v3 on v2

--- a/solution.py
+++ b/solution.py
@@ -20,7 +20,7 @@
 
 def kernel(
     dy_ref, x_ref, pre_ref, wi_ref, wd_ref,
-    dyf_ref, xf_ref, dpre_ref, fina_ref, finb_ref, own_ref, dwd_ref,
+    dyf_ref, xf_ref, dpre_ref, hi_ref, lo_ref, mid_ref, early_ref, base_ref, dwd_ref,
     wd_v, wi_v, dp_v, dyb, preb, prt_v, lin_v, out_v, rs_v, fin_v, acc_v,
     link_s, link_r, d2d_s, d2d_r, push_s, push_r, rs_s, rs_r, load_s, dpre_s, misc_s, dwd_s,
 ):
@@ -29,6 +29,7 @@
     z, c = me // 2, me % 2
     rows, d_model = dy_ref.shape
     short = max(16, rows * 2 // 11 // 16 * 16)
+    part = early_ref.shape[0]
     sizes = ((rows // 2, rows - rows // 2), (rows - short, short))
     ff = wd_ref.shape[0]
     ins, fulls = (dy_ref, x_ref), (dyf_ref, xf_ref)
@@ -87,10 +88,12 @@
             src_ref=out_v, dst_ref=prt_v.at[zb], send_sem=push_s, recv_sem=push_r.at[zb],
             device_id=(g, partner), device_id_type=MESH)
 
-    def rs(d, s, to):
+    def rs(k, src=None, to=None):
+        dst = {4: lin_v.at[4, pl.ds(part, rows - part)], 5: early_ref}.get(k)
+        dst = lin_v.at[k] if dst is None else dst
         return pltpu.make_async_remote_copy(
-            src_ref=rs_v.at[s - 2], dst_ref=lin_v.at[d, s - 2], send_sem=rs_s.at[s - 2], recv_sem=rs_r.at[d, s - 2],
-            device_id=(g, to), device_id_type=MESH)
+            src_ref=dst if src is None else src, dst_ref=dst, send_sem=rs_s.at[k], recv_sem=rs_r.at[k],
+            device_id=(g, partner if to is None else to), device_id_type=MESH)
 
     def local(src, dst, sem):
         return pltpu.make_async_copy(src, dst, sem)
@@ -108,7 +111,7 @@
 
         lax.fori_loop(0, ff // t, body, 0)
 
-    def dx_block(b, store, adds):
+    def dx_block(b, store, adds, tail=None):
         t = tile(d_model)
         at = pl.ds(pl.multiple_of(b * rows, 16), rows)
 
@@ -118,6 +121,8 @@
             for add in adds:
                 acc = acc + add[:, cols].astype(F32)
             store[:, cols] = acc.astype(store.dtype)
+            if tail is not None:
+                store[pl.ds(part, rows - part), cols] += tail[pl.ds(part, rows - part), cols].astype(F32)
             return 0
 
         lax.fori_loop(0, d_model // t, body, 0)
@@ -155,11 +160,6 @@
         dx_block(2 * zb + 1 - c, out_v, ())
         push(zb).start()
 
-    def finish(ref):
-        copy = local(fin_v, ref, misc_s.at[3])
-        copy.start()
-        copy.wait()
-
     def dw_down_rows(m):
         t, tn = tile(ff), 512 if d_model % 512 == 0 else tile(d_model)
         cols = pl.ds(m * t, t)
@@ -212,18 +212,27 @@
     def chip_at(d, s):
         return z + s * (2 * d - 1)
 
-    def sum_at(d, s, lin, ref=None):
+    def sum_at(d, s, store, lin=None):
         zb = chip_at(d, s)
         push(zb).wait_recv()
         adds = [prt_v.at[zb]]
-        if lin:
-            rs(d, s + 1, partner).wait_recv()
-            adds.append(lin_v.at[d, s - 1])
-        dx_block(2 * zb + c, fin_v if s == 1 else rs_v.at[s - 2], adds)
-        if s == 1:
-            finish(ref)
-        else:
-            rs(d, s, 2 * chip_at(d, 1) + c).start()
+        if lin is not None:
+            rs(lin).wait_recv()
+            adds.append(lin_v.at[lin])
+        dx_block(2 * zb + c, store, adds)
+
+    def base(adds, tail=None):
+        push(z).wait_recv()
+        dx_block(2 * z + c, base_v, [prt_v.at[z]] + adds, tail)
+        local(base_v, base_ref, misc_s.at[4]).start()
+
+    base_v = acc_v.at[pl.ds(0, rows)]
+    onward, back = 2 * chip_at(main, 1) + c, 2 * chip_at(other, 1) + c
+    early = c == 1
+    hi_copy = local(rs_v.at[1, pl.ds(part, rows - part)], hi_ref, misc_s.at[3])
+    lo_copy = local(rs_v.at[1, pl.ds(0, part)], lo_ref, misc_s.at[0])
+    mid_copy = local(fin_v.at[pl.ds(0, part)], mid_ref, misc_s.at[1])
+    zero_copy = local(out_v.at[pl.ds(0, part)], early_ref, misc_s.at[5])
 
     barrier = pltpu.get_barrier_semaphore()
     pl.semaphore_signal(barrier, inc=1, device_id=(g, partner), device_id_type=MESH)
@@ -259,11 +268,6 @@
     copy = local(fin_v, xf_ref.at[block(z, c)], misc_s.at[3])
     copy.start()
     copy.wait()
-    push(z).wait_recv()
-    own_v = acc_v.at[pl.ds(0, rows)]
-    dx_block(2 * z + c, own_v, (prt_v.at[z],))
-    local(own_v, own_ref, misc_s.at[4]).start()
-
     for h in range(2):
         for d in range(2):
             @pl.when(arrives(d, 0))
@@ -284,10 +288,6 @@
 
     lax.fori_loop(0, jnp.where(end, 1, 2), near, 0)
 
-    @pl.when(end)
-    def _():
-        sum_at(main, 1, False, fina_ref)
-
     for h in range(2):
         for d in range(2):
             @pl.when(arrives(d, 1))
@@ -312,7 +312,8 @@
 
     @pl.when(end)
     def _():
-        sum_at(main, 2, False)
+        sum_at(main, 2, rs_v.at[0])
+        rs(0, rs_v.at[0], onward).start()
 
     x_in(1, 1, 0)
     x_in(2, 0, 0)
@@ -325,16 +326,20 @@
                 def _():
                     arrival(0, d, 2, h)
         process(3 - z)
-        sum_at(main, 3, False)
+        sum_at(main, 3, rs_v.at[1])
+        rs(1, rs_v.at[1], onward).start()
+        sum_at(main, 1, fin_v)
+        rs(3, fin_v, onward).start()
 
     x_in(1, 0, 0)
     x_in(2, 1, 0)
 
     @pl.when(mid)
     def _():
-        sum_at(main, 1, True, finb_ref)
-
-    local(own_v, own_ref, misc_s.at[4]).wait()
+        sum_at(main, 1, fin_v, 0)
+        rs(4, fin_v.at[pl.ds(part, rows - part)], onward).start()
+        mid_copy.start()
+
     pieces = list(range(ff // tile(ff)))
     dw_down_rows(pieces.pop(0))
 
@@ -345,7 +350,8 @@
 
     @pl.when(mid)
     def _():
-        sum_at(main, 2, True)
+        sum_at(main, 2, rs_v.at[0], 1)
+        rs(2, rs_v.at[0], onward).start()
 
     if pieces:
         dw_down_rows(pieces.pop(0))
@@ -356,7 +362,31 @@
 
     @pl.when(mid)
     def _():
-        sum_at(other, 1, True, fina_ref)
+        sum_at(other, 1, rs_v.at[1], 2)
+        hi_copy.start()
+
+        @pl.when(early)
+        def _():
+            rs(5, rs_v.at[1, pl.ds(0, part)], back).start()
+
+        @pl.when(jnp.logical_not(early))
+        def _():
+            lo_copy.start()
+
+        for k in (3, 4):
+            rs(k).wait_recv()
+        base([lin_v.at[3]], lin_v.at[4])
+
+    @pl.when(end)
+    def _():
+        base([])
+
+    push(z).wait_send()
+
+    @pl.when(mid | jnp.logical_not(early))
+    def _():
+        out_v[pl.ds(0, part), :] = jnp.zeros((part, d_model), BF16)
+        zero_copy.start()
 
     x_in(0, 0, 2)
     x_in(3, 1, 2)
@@ -375,13 +405,36 @@
                 def _():
                     for h in range(2):
                         link(a, d, s, h, z).wait_send()
-    push(z).wait_send()
-    rs(main, 2, partner).wait_send()
+
+    @pl.when(mid | jnp.logical_not(early))
+    def _():
+        zero_copy.wait()
 
     @pl.when(end)
     def _():
-        rs(main, 3, partner).wait_send()
-
+        for k, src in ((0, rs_v.at[0]), (1, rs_v.at[1]), (3, fin_v)):
+            rs(k, src).wait_send()
+
+        @pl.when(early)
+        def _():
+            rs(5).wait_recv()
+
+    @pl.when(mid)
+    def _():
+        for k in (2, 4):
+            rs(k).wait_send()
+        hi_copy.wait()
+        mid_copy.wait()
+
+        @pl.when(early)
+        def _():
+            rs(5).wait_send()
+
+        @pl.when(jnp.logical_not(early))
+        def _():
+            lo_copy.wait()
+
+    local(base_v, base_ref, misc_s.at[4]).wait()
     for b in range(2 * CHIPS):
         dpre_out(b).wait()
     for m in range(ff // tile(ff)):
@@ -393,14 +446,16 @@
     tokens, ff = pre.shape
     out = jax.ShapeDtypeStruct
     dma = pltpu.SemaphoreType.DMA
+    part = max(16, rows * 7 // 22 // 16 * 16)
     flops = 6 * tokens * d_model * ff
     return pl.pallas_call(
         kernel,
         out_shape=(out((tokens, d_model), BF16), out((tokens, d_model), BF16), out((tokens, ff), BF16),
-                   out((rows, d_model), BF16), out((rows, d_model), BF16), out((rows, d_model), F32),
+                   out((rows - part, d_model), BF16), out((part, d_model), BF16), out((part, d_model), BF16),
+                   out((part, d_model), BF16), out((rows, d_model), F32),
                    out((ff, d_model), BF16)),
         in_specs=[pl.BlockSpec(memory_space=pl.ANY)] * 5,
-        out_specs=(pl.BlockSpec(memory_space=pl.ANY),) * 7,
+        out_specs=(pl.BlockSpec(memory_space=pl.ANY),) * 9,
         scratch_shapes=[
             pltpu.VMEM((ff, d_model), BF16),
             pltpu.VMEM((d_model, ff), BF16),
@@ -408,13 +463,13 @@
             pltpu.VMEM((2, rows, d_model), BF16),
             pltpu.VMEM((2, rows, ff), BF16),
             pltpu.VMEM((CHIPS, rows, d_model), BF16),
-            pltpu.VMEM((2, 2, rows, d_model), BF16),
+            pltpu.VMEM((5, rows, d_model), BF16),
             pltpu.VMEM((rows, d_model), BF16),
             pltpu.VMEM((2, rows, d_model), BF16),
             pltpu.VMEM((rows, d_model), BF16),
             pltpu.VMEM((max(rows, tile(ff)), d_model), F32),
             dma((2, 2, 3, 2)), dma((2, 2, 3, 2)), dma((2, CHIPS, 2)), dma((2, CHIPS, 2)),
-            dma, dma((CHIPS,)), dma((2,)), dma((2, 2)), dma((2, 2)), dma((2 * CHIPS,)), dma((5,)), dma((ff // tile(ff),)),
+            dma, dma((CHIPS,)), dma((6,)), dma((6,)), dma((2, 2)), dma((2 * CHIPS,)), dma((6,)), dma((ff // tile(ff),)),
         ],
         compiler_params=pltpu.CompilerParams(
             collective_id=0, has_side_effects=True, vmem_limit_bytes=66_000_000),
@@ -439,12 +494,14 @@
 
 def solution(mesh):
     def step(x, dy, pre, w_in, w_down):
-        _, xf, d_pre, fin_a, fin_b, own, dw_down = gather_and_sum(dy, x, pre, w_in, w_down)
-        a = lax.ppermute(fin_a, "tp", [(i, i ^ 2) for i in range(2 * CHIPS)])
-        b = lax.ppermute(fin_b, "tp", [(i, i ^ 6) for i in range(2, 6)])
+        _, xf, d_pre, hi, lo, mid, early, base, dw_down = gather_and_sum(dy, x, pre, w_in, w_down)
+        hi = lax.ppermute(hi, "tp", [(2, 0), (3, 1), (4, 6), (5, 7)])
+        lo = lax.ppermute(lo, "tp", [(2, 0), (4, 6)])
+        mid = lax.ppermute(mid, "tp", [(2, 4), (3, 5), (4, 2), (5, 3)])
         dw_down = copied(dw_down)
         dw_in = lax.dot_general(xf, d_pre, TN, preferred_element_type=F32).astype(BF16)
-        dx = (own + a.astype(F32) + b.astype(F32)).astype(BF16)
+        lo = early.astype(F32) + lo.astype(F32) + mid.astype(F32)
+        dx = (base + jnp.concatenate([lo, hi.astype(F32)])).astype(BF16)
         return dx, dw_in, dw_down
 
     rows = P(("dp", "tp"), None)

time: 339 us -> 334 us (0.985)
  waiting for transfers between devices: 12.7 us -> 7.21 us
  local copies, waits for them, and re-layouts: 3.69 us -> 0.02 us
    ppermute x2 -> x3, waiting for transfers between devices: 12.7 us -> 7.21 us  [the longest x1 7.2 us: step(): hi = lax.ppermute(hi, 'tp', [(2, 0), (3, 1), (4, 6), (5, 7)])]
    unnamed x8, local copies, waits for them, and re-layouts: 3.69 us -> 0.02 us
  transfers between devices with their start and end apart: 2 -> 3, of which waited for: 1 -> 1; matrix products, arithmetic and copies ran while one was open for 8% -> 9% of each run, Pallas kernels for 1% -> 1%
where the time goes in v3:
time: 334 us
  Pallas kernels  291 us (87%)
  matrix products  28.9 us (9%)
  waiting for transfers between devices  7.21 us (2%)
    pallas_call x1, Pallas kernels, gather_and_sum(): pl.pallas_call(kernel, out_shape=(out((tokens, d_model), BF16), out((toke...  287 us
    dot_general x1, matrix products, step(): lax.dot_general(xf, d_pre, TN, preferred_element_type=F32).astype(BF16)  28.9 us
    ppermute x1, waiting for transfers between devices, step(): hi = lax.ppermute(hi, 'tp', [(2, 0), (3, 1), (4, 6), (5, 7)])  7.2 us
  transfers between devices with their start and end apart: 3, of which 1 were waited for; matrix products, arithmetic and copies ran while one was open for 9% of the time, Pallas kernels for 1%

profile of v3, /device:TPU:0, one launch (start us, length us, event | category | flops | bytes accessed | tf_op | source)
XLA Modules:
  0.0 334.1 jit_solution(11386393813186486671)
XLA Ops:
  0.6 286.8 %gather_and_sum.1 = (bf16[2816,3072]{1,0:T(8,128)(2,1)}, bf16[2816,3072]{1,0:T(8,128)(2,1)}, bf16[2816,1152]{1,0:T(8,128)(2,1)}, bf16[240,3072]{1,0:T(8,128)(2,1...) custom-call(bf16[352,3072]{1,0:T(8,128)(2,1)} %dy_ref.1, ...), custom_call_target="tpu_custom_call" | custom-call | flops 59793997824 | bytes 69206016 | tf_op jit(solution)/shard_map/gather_and_sum/pallas_call | solution.py:451
  287.4 1.3 collective-permute-start
  288.7 0.7 collective-permute-start.1
  289.4 1.3 collective-permute-start.2
  290.7 0.0 copy-start
  290.7 28.9 %convolution_convert_fusion = bf16[3072,1152]{1,0:T(8,128)(2,1)} fusion(bf16[2816,3072]{1,0:T(8,128)(2,1)} %get-tuple-element.16, bf16[2816,1152]{1,0:T(8,128)(2,1)} %get-tuple-element.17), kind=kOutput, calls=%fused_computation | convolution fusion | flops 19934871552 | bytes 30867456 | tf_op jit(solution)/shard_map/dot_general | solution.py:502
  319.7 0.0 slice-start
  319.7 0.0 copy-done
  319.7 0.0 copy-start.1
  319.7 0.0 slice-start.1
  319.7 4.7 %copied.1 = bf16[1152,3072]{1,0:T(8,128)(2,1)} custom-call(bf16[1152,3072]{1,0:T(8,128)(2,1)S(1)} %copy-done), custom_call_target="tpu_custom_call" | custom-call | flops 1769472000 | bytes 14155776 | tf_op jit(solution)/shard_map/copied/pallas_call | solution.py:488
  324.4 0.0 collective-permute-done
  324.4 0.0 collective-permute-done.1
  324.4 0.0 copy-done.1
  324.4 0.3 convert_add_fusion
  324.6 7.2 %collective-permute-done.2 = bf16[240,3072]{1,0:T(8,128)(2,1)S(1)} collective-permute-done((bf16[240,3072]{1,0:T(8,128)(2,1)}, bf16[240,3072]{1,0:T(8,128)(2,1)S(1)}, u32[]{:S(2)}, u32[]{:S(2)}) %collective-permute-start.2) | collective-permute-done | bytes 1474592 | tf_op jit(solution)/shard_map/ppermute | solution.py:498
  331.8 0.3 convert_element_type.21
  332.2 0.0 slice-done
  332.2 0.0 slice-done.1
  332.2 1.9 fusion
  (1 shorter events, 0.0 us)
Async XLA Ops:
  287.4 37.0 %collective-permute-start = (bf16[112,3072]{1,0:T(8,128)(2,1)}, bf16[112,3072]{1,0:T(8,128)(2,1)S(1)}, u32[]{:S(2)}, u32[]{:S(2)}) collective-permute-start(bf16[112,3072]{1,0:T(8,128)(2,1)} %get-tuple-element.13), channel_id=1, source_target_pairs={{2,0},{4,6},{10,8},{12,14},{18,16},{20,22},{26,24},{28,30}} | collective-permute-start | bytes 2064392 | tf_op jit(solution)/shard_map/ppermute | solution.py:499
  288.7 35.7 %collective-permute-start.1 = (bf16[112,3072]{1,0:T(8,128)(2,1)}, bf16[112,3072]{1,0:T(8,128)(2,1)S(1)}, u32[]{:S(2)}, u32[]{:S(2)}) collective-permute-start(bf16[112,3072]{1,0:T(8,128)(2,1)} %get-tuple-element.14), channel_id=1, source_target_pairs={{2,4},{3,5},{4,2},{5,3},{10,12},{11,13},{12,10},{13,11},{18,20},{1... | collective-permute-start | bytes 2064392 | tf_op jit(solution)/shard_map/ppermute | solution.py:500
  289.4 42.4 %collective-permute-start.2 = (bf16[240,3072]{1,0:T(8,128)(2,1)}, bf16[240,3072]{1,0:T(8,128)(2,1)S(1)}, u32[]{:S(2)}, u32[]{:S(2)}) collective-permute-start(bf16[240,3072]{1,0:T(8,128)(2,1)} %get-tuple-element.15), channel_id=1, source_target_pairs={{2,0},{3,1},{4,6},{5,7},{10,8},{11,9},{12,14},{13,15},{18,16},{19,... | collective-permute-start | bytes 4423688 | tf_op jit(solution)/shard_map/ppermute | solution.py:498
  290.7 28.9 %copy-start = (bf16[1152,3072]{1,0:T(8,128)(2,1)S(1)}, bf16[1152,3072]{1,0:T(8,128)(2,1)}, u32[]{:S(2)}) copy-start(bf16[1152,3072]{1,0:T(8,128)(2,1)} %get-tuple-element.18.src) | copy-start | bytes 21233668
  319.7 12.5 %slice-start = ((s8[4325376]{0:T(1024)(128)(4,1)}), s8[4194304]{0:T(1024)(128)(4,1)S(1)}, s32[]{:S(2)}) async-start(s8[4325376]{0:T(1024)(128)(4,1)} %bitcast.2), calls=%async_computation | async-start | bytes 8388608
  319.7 4.7 %copy-start.1 = (bf16[112,3072]{1,0:T(8,128)(2,1)S(1)}, bf16[112,3072]{1,0:T(8,128)(2,1)}, u32[]{:S(2)}) copy-start(bf16[112,3072]{1,0:T(8,128)(2,1)} %get-tuple-element.12) | copy-start | bytes 2064388
  319.7 12.5 %slice-start.1 = ((s8[4325376]{0:T(1024)(128)(4,1)}), s8[131072]{0:T(1024)(128)(4,1)S(1)}, s32[]{:S(2)}) async-start(s8[4325376]{0:T(1024)(128)(4,1)} %bitcast.2), calls=%async_computation.1 | async-start | bytes 262144
